TPU v7x, 32 devices: a whole 2x2x4 slice. The times are simulated.
32 devices in a mesh: beam: 8 (over y, x, core), tm: 4 (over z).
Axes of the slice: x: 2, y: 2, z: 4, core: 2. Of those that a mesh axis runs over, the one named last changes fastest.
Arguments:
- samples: float32 [2, 18874368], P(None, ('beam', 'tm')), parts along dimension 1, may hold values from -6 to 6
- prototype: float32 [16, 4096], replicated, may hold values from -1.5 to 1.5
Outputs:
- spectra: bfloat16 [2, 6144, 4096], P(None, 'beam', 'tm'), parts along dimension 1
There are 8 independent parts, one for each index of `beam`. A program takes and returns all parts, laid end to end along the dimension named above; an argument that names none is the same for every part. Nothing has to cross between parts.
All inputs are finite; a program needn't handle non-finite values.
Results may differ from a plain program's by a relative error of at most 0.001.
Values may be sent and summed in bfloat16 or wider, within the bound.
A program may use at most 128 MiB of HBM per device.

v0:
```python
import functools
import math

import numpy as np
import jax
import jax.numpy as jnp
from jax import lax
from jax.experimental import pallas as pl
from jax.experimental.pallas import tpu as pltpu
from jax.sharding import PartitionSpec as P

CHANNELS = 4096
TAPS = 16
HOP = 3072
LANES = 128
FIRST = 128
SECOND = CHANNELS // FIRST
ROWS = 2 * CHANNELS // LANES
HOP_ROWS = 2 * HOP // LANES
RIM = TAPS * CHANNELS - HOP
RIM_ROWS = 2 * RIM // LANES
CHUNK = 16
GROUP = 8
MESH = pl.DeviceIdType.MESH


def split_pair(table):
    high = np.asarray(table, np.float32).astype(jnp.bfloat16)
    low = (np.asarray(table, np.float64) - high.astype(np.float64)).astype(jnp.bfloat16)
    return high, low


def first_table():
    b1, a, d = np.meshgrid(np.arange(4), np.arange(32), np.arange(FIRST), indexing="ij")
    angle = 2 * np.pi * ((4 * a + b1) * d % FIRST) / FIRST
    cos, sin = np.cos(angle), np.sin(angle)
    table = np.zeros((4, 32, 2, 2, FIRST))
    table[:, :, 0, 0], table[:, :, 1, 0] = cos, sin
    table[:, :, 0, 1], table[:, :, 1, 1] = -sin, cos
    high, low = split_pair(table.reshape(2 * FIRST, 2 * FIRST))
    return np.concatenate([high, high, low], axis=0)


def middle_table():
    angle = 2 * np.pi * np.outer(np.arange(SECOND), np.arange(FIRST)) / CHANNELS
    return (np.stack([np.cos(angle), np.sin(angle)]) / math.sqrt(CHANNELS)).astype(np.float32)


def second_table():
    angle = 2 * np.pi * (np.outer(np.arange(SECOND), np.arange(SECOND)) % SECOND) / SECOND
    eye = np.eye(GROUP)
    both = np.stack([np.cos(angle), np.sin(angle)])
    table = np.einsum("kcm,tu->kctum", both, eye).reshape(2 * SECOND * GROUP, GROUP * SECOND)
    high, low = split_pair(table)
    return np.concatenate([high, high, low], axis=1)


def split_value(value):
    high = value.astype(jnp.bfloat16)
    low = (value - high.astype(jnp.float32)).astype(jnp.bfloat16)
    return high, low


def partner(me, step, count):
    if count & (count - 1):
        return lax.rem(me + step, count)
    other = me
    bit = 1
    while bit < count:
        if step & bit:
            other = other + bit * (1 - 2 * lax.rem(me // bit, 2))
        bit *= 2
    return other


def kernel(count, frames, x_hbm, proto_hbm, one_hbm, mid_hbm, two_hbm, out_ref,
           ext, raw, spread, proto_ref, one_ref, mid_ref, two_ref, folded, lhs, rhs, staged,
           load_sems, own_sem, rim_sems, head_sems, send_sems, recv_sems):
    me = lax.axis_index("tm")
    chunks = frames // CHUNK
    local_rows = frames * HOP_ROWS
    head_rows = CHUNK * HOP_ROWS
    past_rows = RIM_ROWS - head_rows
    width = CHANNELS // count

    loads = [
        pltpu.make_async_copy(source, target, load_sems.at[at])
        for at, (source, target) in enumerate((
            (proto_hbm, raw),
            (x_hbm, ext.at[pl.ds(RIM_ROWS, local_rows)]),
            (one_hbm, one_ref),
            (mid_hbm, mid_ref),
            (two_hbm, two_ref),
        ))
    ]
    for load in loads:
        load.start()

    barrier = pltpu.get_barrier_semaphore()
    for step in range(1, count):
        pl.semaphore_signal(barrier, inc=1, device_id={"tm": partner(me, step, count)}, device_id_type=MESH)
    pl.semaphore_wait(barrier, count - 1)

    def past_copy():
        return pltpu.make_async_remote_copy(
            src_ref=x_hbm.at[pl.ds(local_rows - past_rows, past_rows)],
            dst_ref=ext.at[pl.ds(head_rows, past_rows)],
            send_sem=rim_sems.at[0],
            recv_sem=rim_sems.at[1],
            device_id={"tm": lax.rem(me + 1, count)},
            device_id_type=MESH,
        )

    def head_copy():
        return pltpu.make_async_remote_copy(
            src_ref=x_hbm.at[pl.ds(0, head_rows)],
            dst_ref=ext.at[pl.ds(RIM_ROWS + local_rows, head_rows)],
            send_sem=head_sems.at[0],
            recv_sem=head_sems.at[1],
            device_id={"tm": lax.rem(me + count - 1, count)},
            device_id_type=MESH,
        )

    @pl.when(me < count - 1)
    def _():
        past_copy().start()

    @pl.when(me > 0)
    def _():
        head_copy().start()

    @pl.when(me == 0)
    def _():
        ext[pl.ds(0, RIM_ROWS), :] = jnp.zeros((RIM_ROWS, LANES), jnp.float32)

    loads[0].wait()
    for row in range(ROWS):
        spread[pl.ds(row * TAPS, TAPS), :] = raw[:, pl.ds(row // 2 * LANES, LANES)]
    for tap in range(TAPS):
        for v in range(ROWS // 8):
            proto_ref[tap, pl.ds(v * 8, 8), :] = spread[pl.ds(v * 8 * TAPS + tap, 8, stride=TAPS), :]
    for load in loads[1:]:
        load.wait()
    order = sorted(range(1, count), key=lambda step: (step < count // 2, step))

    def chunk_step(index, carry):
        late = chunks - 2
        chunk = jnp.where(index < late, index + 2,
                          jnp.where(index == late, 1, jnp.where(index == late + 1, chunks, 0)))

        @pl.when(jnp.logical_and(index == late, me > 0))
        def _():
            past_copy().wait_recv()

        @pl.when(index == late + 1)
        def _():
            head_copy().wait_recv()

        base = chunk * (CHUNK * HOP_ROWS)

        def fold(v, carry):
            taps = [proto_ref[tap, pl.ds(pl.multiple_of(v * 8, 8), 8), :] for tap in range(TAPS)]
            for t in range(CHUNK):
                total = None
                for tap in range(TAPS):
                    start = pl.multiple_of(base + (HOP_ROWS * t + ROWS * tap) + v * 8, 8)
                    term = taps[tap] * ext[pl.ds(start, 8), :]
                    total = term if total is None else total + term
                turn = (t + 1) * HOP % CHANNELS * 2 // LANES // 8
                place = lax.rem(v + turn, ROWS // 8)
                folded[t, pl.ds(pl.multiple_of(place * 8, 8), 8), :] = total
            return carry

        lax.fori_loop(0, ROWS // 8, fold, 0)

        lane = lax.broadcasted_iota(jnp.int32, (ROWS, LANES), 1)
        even = lax.rem(lane // SECOND, 2) == 0
        for pair in range(CHUNK // 2):
            one, other = folded[2 * pair], folded[2 * pair + 1]
            upper = jnp.where(even, one, pltpu.roll(other, SECOND, 1))
            lower = jnp.where(even, pltpu.roll(one, LANES - SECOND, 1), other)
            turned = jnp.concatenate([upper, lower], axis=0).T
            high, low = split_value(turned)
            for side in range(2):
                rows = pl.ds((2 * pair + side) * SECOND, SECOND)
                for half in range(2):
                    start = (2 * half + side) * SECOND
                    piece = high[start:start + SECOND]
                    lhs[rows, pl.ds(half * LANES, LANES)] = piece
                    lhs[rows, pl.ds((2 + half) * LANES, LANES)] = low[start:start + SECOND]
                    lhs[rows, pl.ds((4 + half) * LANES, LANES)] = piece

        cos, sin = mid_ref[0], mid_ref[1]
        results = []
        for group in range(CHUNK // GROUP):
            size = GROUP * SECOND
            section = jnp.dot(lhs[pl.ds(group * size, size), :], one_ref[...],
                              preferred_element_type=jnp.float32)
            for t in range(GROUP):
                real = section[t * SECOND:(t + 1) * SECOND, :FIRST]
                imag = section[t * SECOND:(t + 1) * SECOND, FIRST:]
                for half, value in enumerate((real * cos + imag * sin, imag * cos - real * sin)):
                    high, low = split_value(value)
                    columns = pl.ds(half * FIRST, FIRST)
                    rhs[group, pl.ds(t * SECOND, SECOND), columns] = high
                    rhs[group, pl.ds(size + t * SECOND, SECOND), columns] = low
                    rhs[group, pl.ds(2 * size + t * SECOND, SECOND), columns] = high
            product = jnp.dot(two_ref[...], rhs[group], preferred_element_type=jnp.float32)
            results.append((product[:size, :FIRST] + product[size:, FIRST:],
                            product[:size, FIRST:] - product[size:, :FIRST]))
        for part in range(2):
            for c in range(SECOND):
                block = jnp.concatenate(
                    [results[group][part][c * GROUP:(c + 1) * GROUP] for group in range(CHUNK // GROUP)], axis=0)
                owner, at = divmod(c * FIRST, width)
                staged[chunk, owner, part, :, pl.ds(at, FIRST)] = block.astype(jnp.bfloat16)

        rows = pl.ds(pl.multiple_of(me * frames + chunk * CHUNK, CHUNK), CHUNK)
        for step in order:
            to = partner(me, step, count)
            pltpu.make_async_remote_copy(
                src_ref=staged.at[chunk, to],
                dst_ref=out_ref.at[:, rows, :],
                send_sem=send_sems.at[step - 1],
                recv_sem=recv_sems.at[step - 1],
                device_id={"tm": to},
                device_id_type=MESH,
            ).start()
        pltpu.make_async_copy(staged.at[chunk, me], out_ref.at[:, rows, :], own_sem).start()
        return carry

    total = chunks - 1 + jnp.where(me < count - 1, 1, 0) + jnp.where(me == 0, 1, 0)
    lax.fori_loop(0, total, chunk_step, 0)

    @pl.when(me < count - 1)
    def _():
        past_copy().wait_send()

    @pl.when(me > 0)
    def _():
        head_copy().wait_send()

    def each_range(device, act):
        first, last = device == 0, device == count - 1
        for chosen, skip, size in (
            (first, 0, frames + CHUNK),
            (last, CHUNK, frames - CHUNK),
            (jnp.logical_not(jnp.logical_or(first, last)), CHUNK, frames),
        ):
            @pl.when(chosen)
            def _():
                act(out_ref.at[:, pl.ds(pl.multiple_of(device * frames + skip, CHUNK), size), :])

    each_range(me, lambda rows: pltpu.make_async_copy(rows, rows, own_sem).wait())
    for step in order:
        to = partner(me, step, count)
        source = to if not count & (count - 1) else lax.rem(me + count - step, count)

        def described(rows):
            return pltpu.make_async_remote_copy(
                src_ref=rows, dst_ref=rows, send_sem=send_sems.at[step - 1],
                recv_sem=recv_sems.at[step - 1], device_id={"tm": to}, device_id_type=MESH)

        each_range(me, lambda rows: described(rows).wait_send())
        each_range(source, lambda rows: described(rows).wait_recv())


def local(count, samples, prototype):
    frames = samples.shape[1] // HOP
    rows = samples.shape[1] // LANES
    interleaved = samples.reshape(2, rows, LANES).transpose(1, 0, 2).reshape(2 * rows, LANES)
    one, middle, two = first_table(), middle_table(), second_table()
    in_hbm = pl.BlockSpec(memory_space=pltpu.HBM)
    anywhere = pl.BlockSpec(memory_space=pl.ANY)
    width = CHANNELS // count
    return pl.pallas_call(
        functools.partial(kernel, count, frames),
        out_shape=pltpu.VMEM((2, frames * count, width), jnp.bfloat16),
        in_specs=[in_hbm] * 5,
        out_specs=anywhere,
        scratch_shapes=[
            pltpu.VMEM((RIM_ROWS + 2 * rows + CHUNK * HOP_ROWS, LANES), jnp.float32),
            pltpu.VMEM(prototype.shape, jnp.float32),
            pltpu.VMEM((ROWS * TAPS, LANES), jnp.float32),
            pltpu.VMEM((TAPS, ROWS, LANES), jnp.float32),
            pltpu.VMEM(one.shape, one.dtype),
            pltpu.VMEM(middle.shape, middle.dtype),
            pltpu.VMEM(two.shape, two.dtype),
            pltpu.VMEM((CHUNK, ROWS, LANES), jnp.float32),
            pltpu.VMEM((CHUNK * SECOND, 6 * LANES), jnp.bfloat16),
            pltpu.VMEM((CHUNK // GROUP, 3 * GROUP * SECOND, 2 * FIRST), jnp.bfloat16),
            pltpu.VMEM((frames // CHUNK + 1, count, 2, CHUNK, width), jnp.bfloat16),
            pltpu.SemaphoreType.DMA((5,)),
            pltpu.SemaphoreType.DMA,
            pltpu.SemaphoreType.DMA((2,)),
            pltpu.SemaphoreType.DMA((2,)),
            pltpu.SemaphoreType.DMA((count - 1,)),
            pltpu.SemaphoreType.DMA((count - 1,)),
        ],
        compiler_params=pltpu.CompilerParams(
            collective_id=0, has_side_effects=True, vmem_limit_bytes=60300000
        ),
    )(interleaved, prototype, jnp.asarray(one), jnp.asarray(middle), jnp.asarray(two))


def solution(mesh):
    count = mesh.shape["tm"]
    placed = (P(None, ("beam", "tm")), P())
    return jax.shard_map(
        functools.partial(local, count), mesh=mesh, in_specs=placed,
        out_specs=P(None, "beam", "tm"), check_vma=False,
    )
```

profile of v0, /device:TPU:0, one launch (start us, length us, event | category | flops | bytes accessed | tf_op | source)
XLA Modules:
  0.0 80.4 jit_solution(10437727003304071385)
XLA Ops:
  0.0 78.7 %shard_map.55 = bf16[2,768,1024]{2,1,0:T(8,128)(2,1)S(1)} custom-call(f32[9216,128]{1,0:T(8,128)} %bitcast.5, f32[16,4096]{1,0:T(8,128)} %proto_hbm.1, bf16[768,256]{1,0:T(8,128)(2,1)} %constant.6.clone.one_hbm, f32[2,32,128]{2,1,0:T(8,128)} %constant.7.clone.mid_hbm, bf16[512,768]{1,0:T(8,128)(2,1)} %constant.8.clone.two_hbm), custom_call_target="tpu_custom_call" | custom-call | tf_op jit(solution)/shard_map/pallas_call | solution.py:276
  78.7 1.7 %copy.8 = bf16[2,768,1024]{2,1,0:T(8,128)(2,1)} copy(bf16[2,768,1024]{2,1,0:T(8,128)(2,1)S(1)} %shard_map.55) | data formatting | bytes 6291456
where the time goes:
time: 80.5 us; the launch traced here: 80.4 us
  Pallas kernels  78.7 us (98%)
  local copies, waits for them, and re-layouts  1.67 us (2%)
    pallas_call x1, Pallas kernels, local(): pl.pallas_call(functools.partial(kernel, count, frames), out_shape=pltpu....  78.7 us
    unnamed x1, local copies, waits for them, and re-layouts  1.67 us

commit v1 on v0

--- a/solution.py
+++ b/solution.py
@@ -21,6 +21,7 @@
 RIM_ROWS = 2 * RIM // LANES
 CHUNK = 16
 GROUP = 8
+SCALE = 2.0 ** 24
 MESH = pl.DeviceIdType.MESH
 
 
@@ -59,6 +60,18 @@
     high = value.astype(jnp.bfloat16)
     low = (value - high.astype(jnp.float32)).astype(jnp.bfloat16)
     return high, low
+
+
+def encode(value):
+    square = (value * SCALE) * (value * SCALE)
+    power = square * square
+    return jnp.where(value < 0, -power, power).astype(jnp.bfloat16)
+
+
+def decode(code):
+    power = code.astype(jnp.float32)
+    value = jnp.sqrt(jnp.sqrt(jnp.abs(power))) * (1 / SCALE)
+    return jnp.where(power < 0, -value, value)
 
 
 def partner(me, step, count):
@@ -75,7 +88,7 @@
 
 def kernel(count, frames, x_hbm, proto_hbm, one_hbm, mid_hbm, two_hbm, out_ref,
            ext, raw, spread, proto_ref, one_ref, mid_ref, two_ref, folded, lhs, rhs, staged,
-           load_sems, own_sem, rim_sems, head_sems, send_sems, recv_sems):
+           past_out, past_in, head_out, head_in, load_sems, own_sem, rim_sems, head_sems, send_sems, recv_sems):
     me = lax.axis_index("tm")
     chunks = frames // CHUNK
     local_rows = frames * HOP_ROWS
@@ -83,14 +96,22 @@
     past_rows = RIM_ROWS - head_rows
     width = CHANNELS // count
 
+    near_rows = 3 * head_rows
+
+    def part(first, size):
+        return x_hbm.at[pl.ds(first, size)], ext.at[pl.ds(RIM_ROWS + first, size)]
+
     loads = [
         pltpu.make_async_copy(source, target, load_sems.at[at])
         for at, (source, target) in enumerate((
+            part(local_rows - past_rows, past_rows),
+            part(0, head_rows),
             (proto_hbm, raw),
-            (x_hbm, ext.at[pl.ds(RIM_ROWS, local_rows)]),
+            part(head_rows, near_rows - head_rows),
             (one_hbm, one_ref),
             (mid_hbm, mid_ref),
             (two_hbm, two_ref),
+            part(near_rows, local_rows - past_rows - near_rows),
         ))
     ]
     for load in loads:
@@ -99,12 +120,11 @@
     barrier = pltpu.get_barrier_semaphore()
     for step in range(1, count):
         pl.semaphore_signal(barrier, inc=1, device_id={"tm": partner(me, step, count)}, device_id_type=MESH)
-    pl.semaphore_wait(barrier, count - 1)
 
     def past_copy():
         return pltpu.make_async_remote_copy(
-            src_ref=x_hbm.at[pl.ds(local_rows - past_rows, past_rows)],
-            dst_ref=ext.at[pl.ds(head_rows, past_rows)],
+            src_ref=past_out,
+            dst_ref=past_in,
             send_sem=rim_sems.at[0],
             recv_sem=rim_sems.at[1],
             device_id={"tm": lax.rem(me + 1, count)},
@@ -113,14 +133,20 @@
 
     def head_copy():
         return pltpu.make_async_remote_copy(
-            src_ref=x_hbm.at[pl.ds(0, head_rows)],
-            dst_ref=ext.at[pl.ds(RIM_ROWS + local_rows, head_rows)],
+            src_ref=head_out,
+            dst_ref=head_in,
             send_sem=head_sems.at[0],
             recv_sem=head_sems.at[1],
             device_id={"tm": lax.rem(me + count - 1, count)},
             device_id_type=MESH,
         )
 
+    loads[0].wait()
+    past_out[...] = encode(ext[pl.ds(RIM_ROWS + local_rows - past_rows, past_rows), :])
+    loads[1].wait()
+    head_out[...] = encode(ext[pl.ds(RIM_ROWS, head_rows), :])
+    pl.semaphore_wait(barrier, count - 1)
+
     @pl.when(me < count - 1)
     def _():
         past_copy().start()
@@ -133,28 +159,50 @@
     def _():
         ext[pl.ds(0, RIM_ROWS), :] = jnp.zeros((RIM_ROWS, LANES), jnp.float32)
 
-    loads[0].wait()
+    loads[2].wait()
     for row in range(ROWS):
         spread[pl.ds(row * TAPS, TAPS), :] = raw[:, pl.ds(row // 2 * LANES, LANES)]
     for tap in range(TAPS):
         for v in range(ROWS // 8):
             proto_ref[tap, pl.ds(v * 8, 8), :] = spread[pl.ds(v * 8 * TAPS + tap, 8, stride=TAPS), :]
-    for load in loads[1:]:
-        load.wait()
+    loads[3].wait()
     order = sorted(range(1, count), key=lambda step: (step < count // 2, step))
+    early = [step for step in order if step <= max(1, count // 2)]
+
+    late = chunks - 2
+
+    def chunk_of(index):
+        return jnp.where(index < late, index + 2,
+                         jnp.where(index == late, 1, jnp.where(index == late + 1, chunks, 0)))
+
+    def send(chunk, step):
+        to = partner(me, step, count)
+        rows = pl.ds(pl.multiple_of(me * frames + chunk * CHUNK, CHUNK), CHUNK)
+        pltpu.make_async_remote_copy(
+            src_ref=staged.at[chunk, to],
+            dst_ref=out_ref.at[:, rows, :],
+            send_sem=send_sems.at[step - 1],
+            recv_sem=recv_sems.at[step - 1],
+            device_id={"tm": to},
+            device_id_type=MESH,
+        ).start()
 
     def chunk_step(index, carry):
-        late = chunks - 2
-        chunk = jnp.where(index < late, index + 2,
-                          jnp.where(index == late, 1, jnp.where(index == late + 1, chunks, 0)))
+        chunk = chunk_of(index)
+
+        @pl.when(index == 1)
+        def _():
+            loads[7].wait()
 
         @pl.when(jnp.logical_and(index == late, me > 0))
         def _():
             past_copy().wait_recv()
-
-        @pl.when(index == late + 1)
+            ext[pl.ds(head_rows, past_rows), :] = decode(past_in[...])
+
+        @pl.when(jnp.logical_and(index == late + 1, me < count - 1))
         def _():
             head_copy().wait_recv()
+            ext[pl.ds(RIM_ROWS + local_rows, head_rows), :] = decode(head_in[...])
 
         base = chunk * (CHUNK * HOP_ROWS)
 
@@ -172,6 +220,11 @@
             return carry
 
         lax.fori_loop(0, ROWS // 8, fold, 0)
+
+        @pl.when(index == 0)
+        def _():
+            for load in loads[4:7]:
+                load.wait()
 
         lane = lax.broadcasted_iota(jnp.int32, (ROWS, LANES), 1)
         even = lax.rem(lane // SECOND, 2) == 0
@@ -215,22 +268,21 @@
                 owner, at = divmod(c * FIRST, width)
                 staged[chunk, owner, part, :, pl.ds(at, FIRST)] = block.astype(jnp.bfloat16)
 
+        for step in early:
+            send(chunk, step)
         rows = pl.ds(pl.multiple_of(me * frames + chunk * CHUNK, CHUNK), CHUNK)
-        for step in order:
-            to = partner(me, step, count)
-            pltpu.make_async_remote_copy(
-                src_ref=staged.at[chunk, to],
-                dst_ref=out_ref.at[:, rows, :],
-                send_sem=send_sems.at[step - 1],
-                recv_sem=recv_sems.at[step - 1],
-                device_id={"tm": to},
-                device_id_type=MESH,
-            ).start()
         pltpu.make_async_copy(staged.at[chunk, me], out_ref.at[:, rows, :], own_sem).start()
         return carry
 
+    def late_step(index, carry):
+        for step in order:
+            if step not in early:
+                send(chunk_of(index), step)
+        return carry
+
     total = chunks - 1 + jnp.where(me < count - 1, 1, 0) + jnp.where(me == 0, 1, 0)
     lax.fori_loop(0, total, chunk_step, 0)
+    lax.fori_loop(0, total, late_step, 0)
 
     @pl.when(me < count - 1)
     def _():
@@ -273,6 +325,7 @@
     in_hbm = pl.BlockSpec(memory_space=pltpu.HBM)
     anywhere = pl.BlockSpec(memory_space=pl.ANY)
     width = CHANNELS // count
+    past = RIM_ROWS - CHUNK * HOP_ROWS
     return pl.pallas_call(
         functools.partial(kernel, count, frames),
         out_shape=pltpu.VMEM((2, frames * count, width), jnp.bfloat16),
@@ -290,7 +343,11 @@
             pltpu.VMEM((CHUNK * SECOND, 6 * LANES), jnp.bfloat16),
             pltpu.VMEM((CHUNK // GROUP, 3 * GROUP * SECOND, 2 * FIRST), jnp.bfloat16),
             pltpu.VMEM((frames // CHUNK + 1, count, 2, CHUNK, width), jnp.bfloat16),
-            pltpu.SemaphoreType.DMA((5,)),
+            pltpu.VMEM((past, LANES), jnp.bfloat16),
+            pltpu.VMEM((past, LANES), jnp.bfloat16),
+            pltpu.VMEM((CHUNK * HOP_ROWS, LANES), jnp.bfloat16),
+            pltpu.VMEM((CHUNK * HOP_ROWS, LANES), jnp.bfloat16),
+            pltpu.SemaphoreType.DMA((8,)),
             pltpu.SemaphoreType.DMA,
             pltpu.SemaphoreType.DMA((2,)),
             pltpu.SemaphoreType.DMA((2,)),

time: 80.5 us -> 78.2 us (0.971)
  the two profiles are of different devices: /device:TPU:0 before, /device:TPU:16 now
where the time goes in v1:
time: 78.2 us; the launch traced here: 78 us
  Pallas kernels  76.3 us (98%)
  local copies, waits for them, and re-layouts  1.67 us (2%)
    pallas_call x1, Pallas kernels, local(): pl.pallas_call(functools.partial(kernel, count, frames), out_shape=pltpu....  76.3 us
    unnamed x1, local copies, waits for them, and re-layouts  1.67 us

profile of v1, /device:TPU:16, one launch (start us, length us, event | category | flops | bytes accessed | tf_op | source)
XLA Modules:
  0.0 78.0 jit_solution(14507643137588492538)
XLA Ops:
  0.0 76.3 %shard_map.55 = bf16[2,768,1024]{2,1,0:T(8,128)(2,1)S(1)} custom-call(f32[9216,128]{1,0:T(8,128)} %bitcast.5, f32[16,4096]{1,0:T(8,128)} %proto_hbm.1, bf16[768,256]{1,0:T(8,128)(2,1)} %constant.6.clone.one_hbm, f32[2,32,128]{2,1,0:T(8,128)} %constant.7.clone.mid_hbm, bf16[512,768]{1,0:T(8,128)(2,1)} %constant.8.clone.two_hbm), custom_call_target="tpu_custom_call" | custom-call | tf_op jit(solution)/shard_map/pallas_call | solution.py:329
  76.3 1.7 %copy.8 = bf16[2,768,1024]{2,1,0:T(8,128)(2,1)} copy(bf16[2,768,1024]{2,1,0:T(8,128)(2,1)S(1)} %shard_map.55) | data formatting | bytes 6291456

commit v2 on v1

--- a/solution.py
+++ b/solution.py
@@ -21,7 +21,8 @@
 RIM_ROWS = 2 * RIM // LANES
 CHUNK = 16
 GROUP = 8
-SCALE = 2.0 ** 24
+EAGER = 2
+SCALE = 2.0 ** 12
 MESH = pl.DeviceIdType.MESH
 
 
@@ -63,14 +64,18 @@
 
 
 def encode(value):
-    square = (value * SCALE) * (value * SCALE)
-    power = square * square
+    power = value * SCALE
+    for _ in range(3):
+        power = power * power
     return jnp.where(value < 0, -power, power).astype(jnp.bfloat16)
 
 
 def decode(code):
     power = code.astype(jnp.float32)
-    value = jnp.sqrt(jnp.sqrt(jnp.abs(power))) * (1 / SCALE)
+    value = jnp.abs(power)
+    for _ in range(3):
+        value = jnp.sqrt(value)
+    value = value * (1 / SCALE)
     return jnp.where(power < 0, -value, value)
 
 
@@ -145,16 +150,6 @@
     past_out[...] = encode(ext[pl.ds(RIM_ROWS + local_rows - past_rows, past_rows), :])
     loads[1].wait()
     head_out[...] = encode(ext[pl.ds(RIM_ROWS, head_rows), :])
-    pl.semaphore_wait(barrier, count - 1)
-
-    @pl.when(me < count - 1)
-    def _():
-        past_copy().start()
-
-    @pl.when(me > 0)
-    def _():
-        head_copy().start()
-
     @pl.when(me == 0)
     def _():
         ext[pl.ds(0, RIM_ROWS), :] = jnp.zeros((RIM_ROWS, LANES), jnp.float32)
@@ -223,6 +218,16 @@
 
         @pl.when(index == 0)
         def _():
+            pl.semaphore_wait(barrier, count - 1)
+
+            @pl.when(me < count - 1)
+            def _():
+                past_copy().start()
+
+            @pl.when(me > 0)
+            def _():
+                head_copy().start()
+
             for load in loads[4:7]:
                 load.wait()
 
@@ -270,6 +275,13 @@
 
         for step in early:
             send(chunk, step)
+
+        @pl.when(index < EAGER)
+        def _():
+            for step in order:
+                if step not in early:
+                    send(chunk, step)
+
         rows = pl.ds(pl.multiple_of(me * frames + chunk * CHUNK, CHUNK), CHUNK)
         pltpu.make_async_copy(staged.at[chunk, me], out_ref.at[:, rows, :], own_sem).start()
         return carry
@@ -282,7 +294,7 @@
 
     total = chunks - 1 + jnp.where(me < count - 1, 1, 0) + jnp.where(me == 0, 1, 0)
     lax.fori_loop(0, total, chunk_step, 0)
-    lax.fori_loop(0, total, late_step, 0)
+    lax.fori_loop(EAGER, total, late_step, 0)
 
     @pl.when(me < count - 1)
     def _():

time: 78.2 us -> 77.4 us (0.990)
  Pallas kernels: 76.3 us -> 75.5 us
    pallas_call x1, Pallas kernels: 76.3 us -> 75.5 us  [local(): pl.pallas_call(functools.partial(kernel, count, frames), out_shape=pltpu....]
where the time goes in v2:
time: 77.4 us; the launch traced here: 77.2 us
  Pallas kernels  75.5 us (98%)
  local copies, waits for them, and re-layouts  1.67 us (2%)
    pallas_call x1, Pallas kernels, local(): pl.pallas_call(functools.partial(kernel, count, frames), out_shape=pltpu....  75.5 us
    unnamed x1, local copies, waits for them, and re-layouts  1.67 us

profile of v2, /device:TPU:16, one launch (start us, length us, event | category | flops | bytes accessed | tf_op | source)
XLA Modules:
  0.0 77.2 jit_solution(17621825084314845623)
XLA Ops:
  0.0 75.5 %shard_map.55 = bf16[2,768,1024]{2,1,0:T(8,128)(2,1)S(1)} custom-call(f32[9216,128]{1,0:T(8,128)} %bitcast.5, f32[16,4096]{1,0:T(8,128)} %proto_hbm.1, bf16[768,256]{1,0:T(8,128)(2,1)} %constant.6.clone.one_hbm, f32[2,32,128]{2,1,0:T(8,128)} %constant.7.clone.mid_hbm, bf16[512,768]{1,0:T(8,128)(2,1)} %constant.8.clone.two_hbm), custom_call_target="tpu_custom_call" | custom-call | tf_op jit(solution)/shard_map/pallas_call | solution.py:341
  75.6 1.7 %copy.8 = bf16[2,768,1024]{2,1,0:T(8,128)(2,1)} copy(bf16[2,768,1024]{2,1,0:T(8,128)(2,1)S(1)} %shard_map.55) | data formatting | bytes 6291456

commit v3 on v2

--- a/solution.py
+++ b/solution.py
@@ -19,9 +19,10 @@
 HOP_ROWS = 2 * HOP // LANES
 RIM = TAPS * CHANNELS - HOP
 RIM_ROWS = 2 * RIM // LANES
-CHUNK = 16
+CHUNK = 8
+HEAD = 16
 GROUP = 8
-EAGER = 2
+EAGER = 12
 SCALE = 2.0 ** 12
 MESH = pl.DeviceIdType.MESH
 
@@ -93,15 +94,32 @@
 
 def kernel(count, frames, x_hbm, proto_hbm, one_hbm, mid_hbm, two_hbm, out_ref,
            ext, raw, spread, proto_ref, one_ref, mid_ref, two_ref, folded, lhs, rhs, staged,
-           past_out, past_in, head_out, head_in, load_sems, own_sem, rim_sems, head_sems, send_sems, recv_sems):
+           past_out, past_in, head_out, head_in, load_sems, own_sem, rim_sems, head_sems, send_sems, recv_sems, relay):
     me = lax.axis_index("tm")
     chunks = frames // CHUNK
+    skipped = HEAD // CHUNK
     local_rows = frames * HOP_ROWS
-    head_rows = CHUNK * HOP_ROWS
+    chunk_rows = CHUNK * HOP_ROWS
+    head_rows = HEAD * HOP_ROWS
     past_rows = RIM_ROWS - head_rows
     width = CHANNELS // count
-
-    near_rows = 3 * head_rows
+    free_first = -(-RIM_ROWS // chunk_rows)
+    near_rows = (free_first + 2) * chunk_rows - HOP_ROWS + TAPS * ROWS - RIM_ROWS
+    relayed = count == 4
+    inner = jnp.logical_and(me > 0, me < count - 1)
+
+    barrier = pltpu.get_barrier_semaphore()
+    if relayed:
+        @pl.when(me > 0)
+        def _():
+            pl.semaphore_signal(barrier, inc=1, device_id={"tm": me - 1}, device_id_type=MESH)
+
+        @pl.when(me < count - 1)
+        def _():
+            pl.semaphore_signal(barrier, inc=1, device_id={"tm": me + 1}, device_id_type=MESH)
+    else:
+        for step in range(1, count):
+            pl.semaphore_signal(barrier, inc=1, device_id={"tm": partner(me, step, count)}, device_id_type=MESH)
 
     def part(first, size):
         return x_hbm.at[pl.ds(first, size)], ext.at[pl.ds(RIM_ROWS + first, size)]
@@ -110,9 +128,8 @@
         pltpu.make_async_copy(source, target, load_sems.at[at])
         for at, (source, target) in enumerate((
             part(local_rows - past_rows, past_rows),
-            part(0, head_rows),
             (proto_hbm, raw),
-            part(head_rows, near_rows - head_rows),
+            part(0, near_rows),
             (one_hbm, one_ref),
             (mid_hbm, mid_ref),
             (two_hbm, two_ref),
@@ -122,9 +139,8 @@
     for load in loads:
         load.start()
 
-    barrier = pltpu.get_barrier_semaphore()
-    for step in range(1, count):
-        pl.semaphore_signal(barrier, inc=1, device_id={"tm": partner(me, step, count)}, device_id_type=MESH)
+    def relay_to(other):
+        pl.semaphore_signal(relay, inc=1, device_id={"tm": other}, device_id_type=MESH)
 
     def past_copy():
         return pltpu.make_async_remote_copy(
@@ -148,27 +164,40 @@
 
     loads[0].wait()
     past_out[...] = encode(ext[pl.ds(RIM_ROWS + local_rows - past_rows, past_rows), :])
-    loads[1].wait()
-    head_out[...] = encode(ext[pl.ds(RIM_ROWS, head_rows), :])
     @pl.when(me == 0)
     def _():
         ext[pl.ds(0, RIM_ROWS), :] = jnp.zeros((RIM_ROWS, LANES), jnp.float32)
 
-    loads[2].wait()
+    loads[1].wait()
     for row in range(ROWS):
         spread[pl.ds(row * TAPS, TAPS), :] = raw[:, pl.ds(row // 2 * LANES, LANES)]
     for tap in range(TAPS):
         for v in range(ROWS // 8):
             proto_ref[tap, pl.ds(v * 8, 8), :] = spread[pl.ds(v * 8 * TAPS + tap, 8, stride=TAPS), :]
-    loads[3].wait()
+    pl.semaphore_wait(barrier, jnp.where(inner, 2, 1) if relayed else count - 1)
+
+    @pl.when(me < count - 1)
+    def _():
+        past_copy().start()
+
+    if relayed:
+        @pl.when(inner)
+        def _():
+            relay_to(me - 1)
+            relay_to(me + 1)
+
+    loads[2].wait()
     order = sorted(range(1, count), key=lambda step: (step < count // 2, step))
     early = [step for step in order if step <= max(1, count // 2)]
 
-    late = chunks - 2
+    free = chunks - free_first
+    middle = free_first - skipped
 
     def chunk_of(index):
-        return jnp.where(index < late, index + 2,
-                         jnp.where(index == late, 1, jnp.where(index == late + 1, chunks, 0)))
+        return jnp.where(index < free, index + free_first,
+                         jnp.where(index < free + middle, index - free + skipped,
+                                   jnp.where(index < free + middle + skipped, index - free - middle + chunks,
+                                             index - free - middle - skipped)))
 
     def send(chunk, step):
         to = partner(me, step, count)
@@ -185,21 +214,21 @@
     def chunk_step(index, carry):
         chunk = chunk_of(index)
 
-        @pl.when(index == 1)
-        def _():
-            loads[7].wait()
-
-        @pl.when(jnp.logical_and(index == late, me > 0))
+        @pl.when(index == 2)
+        def _():
+            loads[6].wait()
+
+        @pl.when(jnp.logical_and(index == free, me > 0))
         def _():
             past_copy().wait_recv()
             ext[pl.ds(head_rows, past_rows), :] = decode(past_in[...])
 
-        @pl.when(jnp.logical_and(index == late + 1, me < count - 1))
+        @pl.when(jnp.logical_and(index == free + middle, me < count - 1))
         def _():
             head_copy().wait_recv()
             ext[pl.ds(RIM_ROWS + local_rows, head_rows), :] = decode(head_in[...])
 
-        base = chunk * (CHUNK * HOP_ROWS)
+        base = chunk * chunk_rows
 
         def fold(v, carry):
             taps = [proto_ref[tap, pl.ds(pl.multiple_of(v * 8, 8), 8), :] for tap in range(TAPS)]
@@ -218,17 +247,7 @@
 
         @pl.when(index == 0)
         def _():
-            pl.semaphore_wait(barrier, count - 1)
-
-            @pl.when(me < count - 1)
-            def _():
-                past_copy().start()
-
-            @pl.when(me > 0)
-            def _():
-                head_copy().start()
-
-            for load in loads[4:7]:
+            for load in loads[3:6]:
                 load.wait()
 
         lane = lax.broadcasted_iota(jnp.int32, (ROWS, LANES), 1)
@@ -273,14 +292,29 @@
                 owner, at = divmod(c * FIRST, width)
                 staged[chunk, owner, part, :, pl.ds(at, FIRST)] = block.astype(jnp.bfloat16)
 
-        for step in early:
-            send(chunk, step)
-
-        @pl.when(index < EAGER)
-        def _():
-            for step in order:
-                if step not in early:
-                    send(chunk, step)
+        if relayed:
+            @pl.when(jnp.logical_and(index < EAGER, inner))
+            def _():
+                send(chunk, 3)
+
+            @pl.when(index == 0)
+            def _():
+                pl.semaphore_wait(relay, 1)
+
+                @pl.when(inner)
+                def _():
+                    relay_to(jnp.where(me == 1, 0, count - 1))
+
+            send(chunk, 2)
+            send(chunk, 1)
+        else:
+            for step in early:
+                send(chunk, step)
+
+        @pl.when(jnp.logical_and(index == 0, me > 0))
+        def _():
+            head_out[...] = encode(ext[pl.ds(RIM_ROWS, head_rows), :])
+            head_copy().start()
 
         rows = pl.ds(pl.multiple_of(me * frames + chunk * CHUNK, CHUNK), CHUNK)
         pltpu.make_async_copy(staged.at[chunk, me], out_ref.at[:, rows, :], own_sem).start()
@@ -292,9 +326,14 @@
                 send(chunk_of(index), step)
         return carry
 
-    total = chunks - 1 + jnp.where(me < count - 1, 1, 0) + jnp.where(me == 0, 1, 0)
+    total = free + middle + jnp.where(me < count - 1, skipped, 0) + jnp.where(me == 0, skipped, 0)
     lax.fori_loop(0, total, chunk_step, 0)
-    lax.fori_loop(EAGER, total, late_step, 0)
+    if relayed:
+        @pl.when(jnp.logical_not(inner))
+        def _():
+            pl.semaphore_wait(relay, 1)
+
+    lax.fori_loop(jnp.where(inner, EAGER, 0) if relayed else 0, total, late_step, 0)
 
     @pl.when(me < count - 1)
     def _():
@@ -307,9 +346,9 @@
     def each_range(device, act):
         first, last = device == 0, device == count - 1
         for chosen, skip, size in (
-            (first, 0, frames + CHUNK),
-            (last, CHUNK, frames - CHUNK),
-            (jnp.logical_not(jnp.logical_or(first, last)), CHUNK, frames),
+            (first, 0, frames + HEAD),
+            (last, HEAD, frames - HEAD),
+            (jnp.logical_not(jnp.logical_or(first, last)), HEAD, frames),
         ):
             @pl.when(chosen)
             def _():
@@ -337,14 +376,14 @@
     in_hbm = pl.BlockSpec(memory_space=pltpu.HBM)
     anywhere = pl.BlockSpec(memory_space=pl.ANY)
     width = CHANNELS // count
-    past = RIM_ROWS - CHUNK * HOP_ROWS
+    past = RIM_ROWS - HEAD * HOP_ROWS
     return pl.pallas_call(
         functools.partial(kernel, count, frames),
         out_shape=pltpu.VMEM((2, frames * count, width), jnp.bfloat16),
         in_specs=[in_hbm] * 5,
         out_specs=anywhere,
         scratch_shapes=[
-            pltpu.VMEM((RIM_ROWS + 2 * rows + CHUNK * HOP_ROWS, LANES), jnp.float32),
+            pltpu.VMEM((RIM_ROWS + 2 * rows + HEAD * HOP_ROWS, LANES), jnp.float32),
             pltpu.VMEM(prototype.shape, jnp.float32),
             pltpu.VMEM((ROWS * TAPS, LANES), jnp.float32),
             pltpu.VMEM((TAPS, ROWS, LANES), jnp.float32),
@@ -354,17 +393,18 @@
             pltpu.VMEM((CHUNK, ROWS, LANES), jnp.float32),
             pltpu.VMEM((CHUNK * SECOND, 6 * LANES), jnp.bfloat16),
             pltpu.VMEM((CHUNK // GROUP, 3 * GROUP * SECOND, 2 * FIRST), jnp.bfloat16),
-            pltpu.VMEM((frames // CHUNK + 1, count, 2, CHUNK, width), jnp.bfloat16),
+            pltpu.VMEM(((frames + HEAD) // CHUNK, count, 2, CHUNK, width), jnp.bfloat16),
             pltpu.VMEM((past, LANES), jnp.bfloat16),
             pltpu.VMEM((past, LANES), jnp.bfloat16),
-            pltpu.VMEM((CHUNK * HOP_ROWS, LANES), jnp.bfloat16),
-            pltpu.VMEM((CHUNK * HOP_ROWS, LANES), jnp.bfloat16),
-            pltpu.SemaphoreType.DMA((8,)),
+            pltpu.VMEM((HEAD * HOP_ROWS, LANES), jnp.bfloat16),
+            pltpu.VMEM((HEAD * HOP_ROWS, LANES), jnp.bfloat16),
+            pltpu.SemaphoreType.DMA((7,)),
             pltpu.SemaphoreType.DMA,
             pltpu.SemaphoreType.DMA((2,)),
             pltpu.SemaphoreType.DMA((2,)),
             pltpu.SemaphoreType.DMA((count - 1,)),
             pltpu.SemaphoreType.DMA((count - 1,)),
+            pltpu.SemaphoreType.REGULAR,
         ],
         compiler_params=pltpu.CompilerParams(
             collective_id=0, has_side_effects=True, vmem_limit_bytes=60300000

time: 77.4 us -> 76.3 us (0.986)
  Pallas kernels: 75.5 us -> 74.5 us
    pallas_call x1, Pallas kernels: 75.5 us -> 74.5 us  [local(): pl.pallas_call(functools.partial(kernel, count, frames), out_shape=pltpu....]
where the time goes in v3:
time: 76.3 us; the launch traced here: 76.2 us
  Pallas kernels  74.5 us (98%)
  local copies, waits for them, and re-layouts  1.67 us (2%)
    pallas_call x1, Pallas kernels, local(): pl.pallas_call(functools.partial(kernel, count, frames), out_shape=pltpu....  74.5 us
    unnamed x1, local copies, waits for them, and re-layouts  1.67 us

profile of v3, /device:TPU:16, one launch (start us, length us, event | category | flops | bytes accessed | tf_op | source)
XLA Modules:
  0.0 76.2 jit_solution(2547926266555359801)
XLA Ops:
  0.0 74.5 %shard_map.55 = bf16[2,768,1024]{2,1,0:T(8,128)(2,1)S(1)} custom-call(f32[9216,128]{1,0:T(8,128)} %bitcast.5, f32[16,4096]{1,0:T(8,128)} %proto_hbm.1, bf16[768,256]{1,0:T(8,128)(2,1)} %constant.6.clone.one_hbm, f32[2,32,128]{2,1,0:T(8,128)} %constant.7.clone.mid_hbm, bf16[512,768]{1,0:T(8,128)(2,1)} %constant.8.clone.two_hbm), custom_call_target="tpu_custom_call" | custom-call | tf_op jit(solution)/shard_map/pallas_call | solution.py:380
  74.5 1.7 %copy.8 = bf16[2,768,1024]{2,1,0:T(8,128)(2,1)} copy(bf16[2,768,1024]{2,1,0:T(8,128)(2,1)S(1)} %shard_map.55) | data formatting | bytes 6291456

commit v4 on v3

--- a/solution.py
+++ b/solution.py
@@ -22,7 +22,9 @@
 CHUNK = 8
 HEAD = 16
 GROUP = 8
-EAGER = 12
+EAGER = 15
+LAST = 8
+HELD = 6
 SCALE = 2.0 ** 12
 MESH = pl.DeviceIdType.MESH
 
@@ -92,7 +94,7 @@
     return other
 
 
-def kernel(count, frames, x_hbm, proto_hbm, one_hbm, mid_hbm, two_hbm, out_ref,
+def kernel(count, frames, x_hbm, proto_hbm, one_hbm, mid_hbm, two_hbm, out_ref, tail_ref,
            ext, raw, spread, proto_ref, one_ref, mid_ref, two_ref, folded, lhs, rhs, staged,
            past_out, past_in, head_out, head_in, load_sems, own_sem, rim_sems, head_sems, send_sems, recv_sems, relay):
     me = lax.axis_index("tm")
@@ -320,20 +322,39 @@
         pltpu.make_async_copy(staged.at[chunk, me], out_ref.at[:, rows, :], own_sem).start()
         return carry
 
+    tail_first = chunks + skipped - LAST
+
     def late_step(index, carry):
-        for step in order:
-            if step not in early:
-                send(chunk_of(index), step)
+        chunk = chunk_of(index)
+        if relayed:
+            @pl.when(jnp.logical_or(chunk < tail_first, jnp.logical_not(inner)))
+            def _():
+                send(chunk, 3)
+        else:
+            for step in order:
+                if step not in early:
+                    send(chunk, step)
         return carry
 
     total = free + middle + jnp.where(me < count - 1, skipped, 0) + jnp.where(me == 0, skipped, 0)
     lax.fori_loop(0, total, chunk_step, 0)
     if relayed:
+        @pl.when(inner)
+        def _():
+            lax.fori_loop(EAGER, total, late_step, 0)
+            to = partner(me, 3, count)
+            for at in range(LAST):
+                for part in range(2):
+                    tail_ref[part, pl.ds(at * CHUNK, CHUNK), :] = staged[tail_first + at, to, part]
+
         @pl.when(jnp.logical_not(inner))
         def _():
             pl.semaphore_wait(relay, 1)
-
-    lax.fori_loop(jnp.where(inner, EAGER, 0) if relayed else 0, total, late_step, 0)
+            lax.fori_loop(0, total - HELD, late_step, 0)
+            pl.semaphore_wait(relay, 1)
+            lax.fori_loop(total - HELD, total, late_step, 0)
+    else:
+        lax.fori_loop(0, total, late_step, 0)
 
     @pl.when(me < count - 1)
     def _():
@@ -343,12 +364,12 @@
     def _():
         head_copy().wait_send()
 
-    def each_range(device, act):
+    def each_range(device, act, left=0):
         first, last = device == 0, device == count - 1
         for chosen, skip, size in (
             (first, 0, frames + HEAD),
             (last, HEAD, frames - HEAD),
-            (jnp.logical_not(jnp.logical_or(first, last)), HEAD, frames),
+            (jnp.logical_not(jnp.logical_or(first, last)), HEAD, frames - left),
         ):
             @pl.when(chosen)
             def _():
@@ -358,14 +379,60 @@
     for step in order:
         to = partner(me, step, count)
         source = to if not count & (count - 1) else lax.rem(me + count - step, count)
+        left = LAST * CHUNK if relayed and step == 3 else 0
 
         def described(rows):
             return pltpu.make_async_remote_copy(
                 src_ref=rows, dst_ref=rows, send_sem=send_sems.at[step - 1],
                 recv_sem=recv_sems.at[step - 1], device_id={"tm": to}, device_id_type=MESH)
 
-        each_range(me, lambda rows: described(rows).wait_send())
-        each_range(source, lambda rows: described(rows).wait_recv())
+        each_range(me, lambda rows: described(rows).wait_send(), left)
+        if relayed and step == 2:
+            @pl.when(inner)
+            def _():
+                relay_to(jnp.where(me == 1, 0, count - 1))
+
+        each_range(source, lambda rows: described(rows).wait_recv(), left)
+
+
+def flush(gathered_ref, out_hbm, order_ref, sems):
+    order_ref[...] = jnp.zeros_like(order_ref)
+    copies = [pltpu.make_async_copy(gathered_ref.at[part], out_hbm.at[part], sems.at[part]) for part in range(2)]
+    for copy in copies:
+        copy.start()
+    for copy in copies:
+        copy.wait()
+
+
+def swap(count, tail_ref, order_ref, got_ref, send_sem, recv_sem):
+    me = lax.axis_index("tm")
+
+    @pl.when(jnp.logical_and(me > 0, me < count - 1))
+    def _():
+        other = {"tm": partner(me, 3, count)}
+        barrier = pltpu.get_barrier_semaphore()
+        pl.semaphore_signal(barrier, inc=1, device_id=other, device_id_type=MESH)
+        pl.semaphore_wait(barrier, 1)
+        copy = pltpu.make_async_remote_copy(
+            src_ref=tail_ref, dst_ref=got_ref, send_sem=send_sem, recv_sem=recv_sem,
+            device_id=other, device_id_type=MESH)
+        copy.start()
+        copy.wait()
+
+
+def patch(count, frames, flushed_hbm, got_ref, out_hbm, sems):
+    me = lax.axis_index("tm")
+
+    @pl.when(jnp.logical_and(me > 0, me < count - 1))
+    def _():
+        size = LAST * CHUNK
+        first = partner(me, 3, count) * frames + frames + HEAD - size
+        rows = pl.ds(pl.multiple_of(first, CHUNK), size)
+        copies = [pltpu.make_async_copy(got_ref.at[part], out_hbm.at[part, rows, :], sems.at[part]) for part in range(2)]
+        for copy in copies:
+            copy.start()
+        for copy in copies:
+            copy.wait()
 
 
 def local(count, samples, prototype):
@@ -377,11 +444,13 @@
     anywhere = pl.BlockSpec(memory_space=pl.ANY)
     width = CHANNELS // count
     past = RIM_ROWS - HEAD * HOP_ROWS
-    return pl.pallas_call(
+    whole = (2, frames * count, width)
+    few = (2, LAST * CHUNK, width)
+    gathered, tail = pl.pallas_call(
         functools.partial(kernel, count, frames),
-        out_shape=pltpu.VMEM((2, frames * count, width), jnp.bfloat16),
+        out_shape=(pltpu.VMEM(whole, jnp.bfloat16), pltpu.VMEM(few, jnp.bfloat16)),
         in_specs=[in_hbm] * 5,
-        out_specs=anywhere,
+        out_specs=(anywhere, pl.BlockSpec(memory_space=pltpu.VMEM)),
         scratch_shapes=[
             pltpu.VMEM((RIM_ROWS + 2 * rows + HEAD * HOP_ROWS, LANES), jnp.float32),
             pltpu.VMEM(prototype.shape, jnp.float32),
@@ -410,6 +479,27 @@
             collective_id=0, has_side_effects=True, vmem_limit_bytes=60300000
         ),
     )(interleaved, prototype, jnp.asarray(one), jnp.asarray(middle), jnp.asarray(two))
+    if count != 4:
+        return gathered
+    small = pltpu.CompilerParams(vmem_limit_bytes=2000000)
+    in_vmem = pl.BlockSpec(memory_space=pltpu.VMEM)
+    flushed, ordered = pl.pallas_call(
+        flush, out_shape=(pltpu.HBM(whole, jnp.bfloat16), pltpu.VMEM((8, LANES), jnp.float32)),
+        in_specs=[anywhere], out_specs=(in_hbm, in_vmem),
+        scratch_shapes=[pltpu.SemaphoreType.DMA((2,))], compiler_params=small,
+    )(gathered)
+    got = pl.pallas_call(
+        functools.partial(swap, count), out_shape=pltpu.VMEM(few, jnp.bfloat16),
+        in_specs=[anywhere, anywhere], out_specs=anywhere,
+        scratch_shapes=[pltpu.SemaphoreType.DMA, pltpu.SemaphoreType.DMA],
+        compiler_params=pltpu.CompilerParams(
+            collective_id=1, has_side_effects=True, vmem_limit_bytes=2000000),
+    )(tail, ordered)
+    return pl.pallas_call(
+        functools.partial(patch, count, frames), out_shape=pltpu.HBM(whole, jnp.bfloat16),
+        in_specs=[in_hbm, anywhere], out_specs=in_hbm, input_output_aliases={0: 0},
+        scratch_shapes=[pltpu.SemaphoreType.DMA((2,))], compiler_params=small,
+    )(flushed, got)
 
 
 def solution(mesh):

time: 76.3 us -> 75.7 us (level)
  local copies, waits for them, and re-layouts: 1.67 us -> 0 us
  Pallas kernels: 74.5 us -> 75.5 us
    unnamed x1 -> x0, local copies, waits for them, and re-layouts: 1.67 us -> none
    pallas_call x1 -> x4, Pallas kernels: 74.5 us -> 75.5 us  [the longest x1 64.7 us: local(): pl.pallas_call(functools.partial(kernel, count, frames), out_shape=(pltpu...]
where the time goes in v4:
time: 75.7 us; the launch traced here: 75.6 us
  Pallas kernels  75.5 us (100%)
    pallas_call x1, Pallas kernels, local(): pl.pallas_call(functools.partial(kernel, count, frames), out_shape=(pltpu...  64.7 us
    pallas_call x1, Pallas kernels, local(): pl.pallas_call(functools.partial(swap, count), out_shape=pltpu.VMEM(few,...  8.42 us
    pallas_call x1, Pallas kernels, local(): pl.pallas_call(flush, out_shape=(pltpu.HBM(whole, jnp.bfloat16), pltpu.VM...  1.68 us

profile of v4, /device:TPU:16, one launch (start us, length us, event | category | flops | bytes accessed | tf_op | source)
XLA Modules:
  0.0 75.6 jit_solution(14693448746071975562)
XLA Ops:
  0.0 64.7 %shard_map.55 = (bf16[2,768,1024]{2,1,0:T(8,128)(2,1)S(1)}, bf16[2,64,1024]{2,1,0:T(8,128)(2,1)S(1)}) custom-call(f32[9216,128]{1,0:T(8,128)} %bitcast.5, f32[16,4096]{1,0:T(8,128)} %proto_hbm.1, bf16[768,256]{1,0:T(8,128)(2,1)} %constant.6.clone.one_hbm, f32[2,32,128]{2,1,0:T(8,128)} %constant.7.clone.mid_hbm, bf16[512,768]{1,0:T(8,128)(2,1)} %constant.8.clone.two_hbm), custom_call_target="tpu_custom_call" | custom-call | tf_op jit(solution)/shard_map/pallas_call | solution.py:449
  64.7 1.7 %shard_map.56 = (bf16[2,768,1024]{2,1,0:T(8,128)(2,1)}, f32[8,128]{1,0:T(8,128)S(1)}) custom-call(bf16[2,768,1024]{2,1,0:T(8,128)(2,1)S(1)} %get-tuple-element.9.gathered_ref), custom_call_target="tpu_custom_call" | custom-call | tf_op jit(solution)/shard_map/pallas_call | solution.py:486
  66.4 8.4 %shard_map.57.got_ref = bf16[2,64,1024]{2,1,0:T(8,128)(2,1)S(1)} custom-call(bf16[2,64,1024]{2,1,0:T(8,128)(2,1)S(1)} %get-tuple-element.11.tail_ref, f32[8,128]{1,0:T(8,128)S(1)} %get-tuple-element.12.order_ref), custom_call_target="tpu_custom_call" | custom-call | tf_op jit(solution)/shard_map/pallas_call | solution.py:491
  74.8 0.7 shard_map.58

commit v5 on v4

--- a/solution.py
+++ b/solution.py
@@ -24,7 +24,7 @@
 GROUP = 8
 EAGER = 15
 LAST = 8
-HELD = 6
+HELD = (8, 6)
 SCALE = 2.0 ** 12
 MESH = pl.DeviceIdType.MESH
 
@@ -108,6 +108,8 @@
     free_first = -(-RIM_ROWS // chunk_rows)
     near_rows = (free_first + 2) * chunk_rows - HOP_ROWS + TAPS * ROWS - RIM_ROWS
     relayed = count == 4
+    held = jnp.where(lax.rem(lax.axis_index("beam"), 2) == 0, HELD[0], HELD[1])
+    eager = EAGER - jnp.where(me == 1, lax.rem(lax.axis_index("beam"), 2), 0)
     inner = jnp.logical_and(me > 0, me < count - 1)
 
     barrier = pltpu.get_barrier_semaphore()
@@ -295,7 +297,7 @@
                 staged[chunk, owner, part, :, pl.ds(at, FIRST)] = block.astype(jnp.bfloat16)
 
         if relayed:
-            @pl.when(jnp.logical_and(index < EAGER, inner))
+            @pl.when(jnp.logical_and(index < eager, inner))
             def _():
                 send(chunk, 3)
 
@@ -341,7 +343,7 @@
     if relayed:
         @pl.when(inner)
         def _():
-            lax.fori_loop(EAGER, total, late_step, 0)
+            lax.fori_loop(eager, total, late_step, 0)
             to = partner(me, 3, count)
             for at in range(LAST):
                 for part in range(2):
@@ -350,9 +352,9 @@
         @pl.when(jnp.logical_not(inner))
         def _():
             pl.semaphore_wait(relay, 1)
-            lax.fori_loop(0, total - HELD, late_step, 0)
+            lax.fori_loop(0, total - held, late_step, 0)
             pl.semaphore_wait(relay, 1)
-            lax.fori_loop(total - HELD, total, late_step, 0)
+            lax.fori_loop(total - held, total, late_step, 0)
     else:
         lax.fori_loop(0, total, late_step, 0)
 

time: 75.7 us -> 75.3 us (level)
    pallas_call x1, Pallas kernels: 8.42 us -> 6.66 us  [local(): pl.pallas_call(functools.partial(swap, count), out_shape=pltpu.VMEM(few,...]
    pallas_call x1, Pallas kernels: 64.7 us -> 66.1 us  [local(): pl.pallas_call(functools.partial(kernel, count, frames), out_shape=(pltpu...]
where the time goes in v5:
time: 75.3 us; the launch traced here: 75.2 us
  Pallas kernels  75.2 us (100%)
    pallas_call x1, Pallas kernels, local(): pl.pallas_call(functools.partial(kernel, count, frames), out_shape=(pltpu...  66.1 us
    pallas_call x1, Pallas kernels, local(): pl.pallas_call(functools.partial(swap, count), out_shape=pltpu.VMEM(few,...  6.66 us
    pallas_call x1, Pallas kernels, local(): pl.pallas_call(flush, out_shape=(pltpu.HBM(whole, jnp.bfloat16), pltpu.VM...  1.68 us

profile of v5, /device:TPU:16, one launch (start us, length us, event | category | flops | bytes accessed | tf_op | source)
XLA Modules:
  0.0 75.2 jit_solution(10075847429010813740)
XLA Ops:
  0.0 66.1 %shard_map.55 = (bf16[2,768,1024]{2,1,0:T(8,128)(2,1)S(1)}, bf16[2,64,1024]{2,1,0:T(8,128)(2,1)S(1)}) custom-call(f32[9216,128]{1,0:T(8,128)} %bitcast.5, f32[16,4096]{1,0:T(8,128)} %proto_hbm.1, bf16[768,256]{1,0:T(8,128)(2,1)} %constant.6.clone.one_hbm, f32[2,32,128]{2,1,0:T(8,128)} %constant.7.clone.mid_hbm, bf16[512,768]{1,0:T(8,128)(2,1)} %constant.8.clone.two_hbm), custom_call_target="tpu_custom_call" | custom-call | tf_op jit(solution)/shard_map/pallas_call | solution.py:451
  66.1 1.7 %shard_map.56 = (bf16[2,768,1024]{2,1,0:T(8,128)(2,1)}, f32[8,128]{1,0:T(8,128)S(1)}) custom-call(bf16[2,768,1024]{2,1,0:T(8,128)(2,1)S(1)} %get-tuple-element.9.gathered_ref), custom_call_target="tpu_custom_call" | custom-call | tf_op jit(solution)/shard_map/pallas_call | solution.py:488
  67.8 6.7 %shard_map.57.got_ref = bf16[2,64,1024]{2,1,0:T(8,128)(2,1)S(1)} custom-call(bf16[2,64,1024]{2,1,0:T(8,128)(2,1)S(1)} %get-tuple-element.11.tail_ref, f32[8,128]{1,0:T(8,128)S(1)} %get-tuple-element.12.order_ref), custom_call_target="tpu_custom_call" | custom-call | tf_op jit(solution)/shard_map/pallas_call | solution.py:493
  74.5 0.7 shard_map.58
